TPU v7x, 32 devices: a whole 2x2x4 slice. The times are simulated.
32 devices in a mesh: clip: 2 (over y), ha: 8 (over z, x), ta: 2 (over core).
Axes of the slice: x: 2, y: 2, z: 4, core: 2. Of those that a mesh axis runs over, the one named last changes fastest.
Arguments:
- latent_tokens: bfloat16 [16, 512, 64], P('clip', ('ha', 'ta')), parts along dimension 0, may hold values from -8 to 8
- w_in: bfloat16 [3, 3, 3, 16, 384], replicated, may hold values from -0.3125 to 0.3125
- b_in: float32 [384], replicated, may hold values from -3 to 3
- gn_gain: float32 [384], replicated, may hold values from 0.1 to 1.9
- gn_shift: float32 [384], replicated, may hold values from -3 to 3
- w_mid: bfloat16 [3, 3, 3, 384, 384], replicated, may hold values from -0.109375 to 0.109375
- b_mid: float32 [384], replicated, may hold values from -3 to 3
Outputs:
- decoded: bfloat16 [16, 16, 128, 384], P(('clip', 'ta'), 'ha'), parts along dimension 0
There are 2 independent parts, one for each index of `clip`. A program takes and returns all parts, laid end to end along the dimension named above; an argument that names none is the same for every part. Nothing has to cross between parts.
All inputs are finite; a program needn't handle non-finite values.
Results may differ from a plain program's by a relative error of at most 0.0054.
Values may be sent and summed in bfloat16 or wider, within the bound.
A program may use at most 64 MiB of HBM per device.

v0:
```python
import jax
import jax.numpy as jnp
from jax import lax
from jax.sharding import PartitionSpec as P

GROUPS = 32
H_DEV = 2
W = 128
eps = 1e-06


def passed_along(value, axis, by):
    devices = lax.axis_size(axis)
    pairs = [(i, i + by) for i in range(devices) if 0 <= i + by < devices]
    return lax.ppermute(value, axis, pairs)


def extended_2(value, sides, width):
    for axis, dim in sides:
        devices, length = (lax.axis_size(axis), value.shape[dim])
        up = [(i, (i + 1) % devices) for i in range(devices - 1)]
        down = [(j, i) for i, j in up]
        last = lax.slice_in_dim(value, length - width, length, axis=dim)
        first = lax.slice_in_dim(value, 0, width, axis=dim)
        before = lax.ppermute(last, axis, up)
        after = lax.ppermute(first, axis, down)
        value = jnp.concatenate([before, value, after], axis=dim)
    return value


def unpatch(tokens, rows, cols):
    frames = tokens.shape[0]
    latent_ch = tokens.shape[2] // 4
    blocks = tokens.reshape(frames, rows // 2, cols // 2, 2, 2, latent_ch)
    return blocks.transpose(0, 1, 3, 2, 4, 5).reshape(frames, rows, cols, latent_ch)


def pad_cols(field):
    return jnp.pad(field, ((0, 0), (0, 0), (1, 1), (0, 0)))


def input_conv(padded, w_in, b_in, frames, rows, cols):
    pieces = [
        padded[frame_tap : frame_tap + frames, row_tap : row_tap + rows, col_tap : col_tap + cols]
        for frame_tap in range(3)
        for row_tap in range(3)
        for col_tap in range(3)
    ]
    stacked = jnp.concatenate(pieces, axis=-1).reshape(frames * rows * cols, -1)
    result = jnp.dot(
        stacked, w_in.reshape(stacked.shape[1], -1), preferred_element_type=jnp.float32
    )
    return (result + b_in).reshape(frames, rows, cols, -1)


def middle_conv(padded, w_mid, frames, rows, cols):
    channels = padded.shape[-1]
    total = jnp.zeros((frames * rows * cols, w_mid.shape[-1]), jnp.float32)
    for frame_tap in range(3):
        for row_tap in range(3):
            slab = jnp.concatenate(
                [
                    padded[
                        frame_tap : frame_tap + frames,
                        row_tap : row_tap + rows,
                        col_tap : col_tap + cols,
                    ]
                    for col_tap in range(3)
                ],
                axis=-1,
            ).reshape(frames * rows * cols, 3 * channels)
            total = total + jnp.dot(
                slab,
                w_mid[frame_tap, row_tap].reshape(3 * channels, -1),
                preferred_element_type=jnp.float32,
            )
    return total.reshape(frames, rows, cols, -1)


def group_totals(field):
    grouped = field.reshape(-1, GROUPS, field.shape[-1] // GROUPS)
    return jnp.sum(grouped, axis=(0, 2))


def normalize(hidden, mean, var, gn_gain, gn_shift):
    members = hidden.shape[-1] // GROUPS
    mean_chan = jnp.repeat(mean, members)
    scale_chan = jnp.repeat(lax.rsqrt(var + eps), members)
    scaled = (hidden.astype(jnp.float32) - mean_chan) * scale_chan * gn_gain + gn_shift
    return jax.nn.silu(scaled).astype(jnp.bfloat16)


def body(latent_tokens, w_in, b_in, gn_gain, gn_shift, w_mid, b_mid):
    rows = H_DEV
    cols = W
    moved = lax.all_to_all(latent_tokens, "ta", split_axis=0, concat_axis=1, tiled=True)
    latent = unpatch(moved, rows, cols)
    frames = latent.shape[0]
    earlier = passed_along(latent, "ta", 1)
    extended = jnp.concatenate([earlier, latent], axis=0)
    framed = extended_2(extended, (("ha", 1),), 2)
    wide_hidden = input_conv(pad_cols(framed), w_in, b_in, frames + 2, rows + 2, cols).astype(
        jnp.bfloat16
    )
    hidden = wide_hidden[2:, 1 : rows + 1]
    values = lax.optimization_barrier(hidden).astype(jnp.float32)
    members = values.shape[-1] // GROUPS
    count = float(lax.axis_size("ha") * lax.axis_size("ta") * frames * rows * cols * members)
    mean = lax.psum(group_totals(values), ("ha", "ta")) / count
    centered = values - jnp.repeat(mean, members)
    var = lax.psum(group_totals(centered * centered), ("ha", "ta")) / count
    active = normalize(wide_hidden, mean, var, gn_gain, gn_shift)
    frame_pos = lax.axis_index("ta") * frames + jnp.arange(frames + 2, dtype=jnp.int32) - 2
    row_pos = lax.axis_index("ha") * rows + jnp.arange(rows + 2, dtype=jnp.int32) - 1
    inside = (
        (frame_pos >= 0)[:, None]
        & (row_pos >= 0)[None, :]
        & (row_pos < rows * lax.axis_size("ha"))[None, :]
    )
    padded = jnp.where(inside[:, :, None, None], active, jnp.zeros_like(active))
    branch = middle_conv(pad_cols(padded), w_mid, frames, rows, cols)
    return (values + branch + b_mid).astype(jnp.bfloat16)


def solution(mesh):
    placed = (P("clip", ("ha", "ta"), None), P(), P(), P(), P(), P(), P())
    return jax.shard_map(
        body,
        mesh=mesh,
        in_specs=placed,
        out_specs=P(("clip", "ta"), "ha", None, None),
        check_vma=False,
    )
```

profile of v0, /device:TPU:0, one launch (start us, length us, event | category | flops | bytes accessed | tf_op | source)
XLA Modules:
  0.0 131.4 jit_solution(58256040233946923)
XLA Ops:
  0.0 1.0 reshape.124
  1.0 3.7 %all_to_all.15 = bf16[2,2,4096]{2,1,0:T(2,128)(2,1)S(1)} all-to-all(bf16[2,2,4096]{2,1,0:T(2,128)(2,1)S(1)} %reshape.124), channel_id=1, replica_groups=mesh['clip'=2,'ha'=8,'ta'=2] {'ta'}, dimensions={0} | all-to-all | bytes 65536 | tf_op jit(solution)/shard_map/all_to_all | solution.py:96
  5.1 0.2 copy.15
  5.3 2.1 %collective-permute-start = (bf16[4,2,128,16]{3,2,1,0:T(8,128)(2,1)S(1)}, bf16[4,2,128,16]{3,2,1,0:T(8,128)(2,1)S(1)}, u32[]{:S(2)}, u32[]{:S(2)}) collective-permute-start(bf16[4,2,128,16]{3,2,1,0:T(8,128)(2,1)S(1)} %bitcast.63), channel_id=1, source_target_pairs={{0,1},{2,3},{4,5},{6,7},{8,9},{10,11},{12,13},{14,15},{16,17},{18,... | collective-permute-start | bytes 98312 | tf_op jit(solution)/shard_map/ppermute | solution.py:15
  7.4 5.7 %fusion.25 = (bf16[1,1,3,384,384]{4,3,2,1,0:T(8,128)(2,1)}, bf16[1,1,3,384,384]{4,3,2,1,0:T(8,128)(2,1)}, bf16[1,1,3,384,384]{4,3,2,1,0:T(8,128)(2,1)}, bf16[1,1...) fusion(bf16[3,3,3,384,384]{4,3,2,1,0:T(8,128)(2,1)} %param.12), kind=kLoop, calls=%fused_computation.94 | loop fusion | bytes 15925248 | tf_op jit(solution)/shard_map/slice | solution.py:74
  13.4 1.3 collective-permute-start.2
  14.7 5.5 %collective-permute-start.1 = (bf16[8,2,128,16]{2,3,1,0:T(8,128)(2,1)S(1)}, bf16[8,2,128,16]{2,3,1,0:T(8,128)(2,1)S(1)}, u32[]{:S(2)}, u32[]{:S(2)}) collective-permute-start(bf16[8,2,128,16]{2,3,1,0:T(8,128)(2,1)S(1)} %pad_maximum_fusion.11), channel_id=1, source_target_pairs={{0,2},{2,4},{4,6},{6,8},{8,10},{10,12},{12,14},{1,3},{3,5},{5,7},{... | collective-permute-start | bytes 196616 | tf_op jit(solution)/shard_map/ppermute | solution.py:25
  20.3 0.2 collective-permute-done.2
  20.6 1.6 %collective-permute-done.1 = bf16[8,2,128,16]{2,3,1,0:T(8,128)(2,1)S(1)} collective-permute-done((bf16[8,2,128,16]{2,3,1,0:T(8,128)(2,1)S(1)}, bf16[8,2,128,16]{2,3,1,0:T(8,128)(2,1)S(1)}, u32[]{:S(2)}, u32[]{:S(2)}) %collective-permute-start.1) | collective-permute-done | bytes 65568 | tf_op jit(solution)/shard_map/ppermute | solution.py:25
  24.5 1.0 copy.18
  25.6 3.2 %reshape.112 = bf16[3072,432]{0,1:T(8,128)(2,1)} reshape(bf16[6,4,128,432]{2,1,0,3:T(4,128)(2,1)S(1)} %copy.18) | data formatting | bytes 5308416 | tf_op jit(solution)/shard_map/reshape | solution.py:49
  28.7 3.6 %add_convert_fusion = bf16[3072,384]{1,0:T(8,128)(2,1)S(1)} fusion(bf16[3072,432]{0,1:T(8,128)(2,1)} %reshape.112, bf16[432,384]{1,0:T(8,128)(2,1)S(1)} %bitcast.49, f32[384]{0:T(512)S(1)} %copy-done.14), kind=kOutput, calls=%fused_computation.1 | convolution fusion | flops 1021575168 | bytes 5346816 | tf_op jit(solution)/shard_map/dot_general | solution.py:50
  32.4 0.2 convert_reduce_fusion
  32.8 32.9 %psum.14 = f32[32]{0:T(128)S(1)} all-reduce(f32[32]{0:T(128)S(1)} %reduce_sum.25), channel_id=1, replica_groups=mesh['clip'=2,'ha'=8,'ta'=2] {'ha','ta'}, use_global_device_ids=true, to_apply=%region_2.3 | all-reduce | flops 32 | bytes 256 | tf_op jit(solution)/shard_map/psum | solution.py:109
  66.0 0.3 fusion.2
  66.5 29.7 %psum.15 = f32[32]{0:T(128)S(1)} all-reduce(f32[32]{0:T(128)S(1)} %reduce_sum.37), channel_id=1, replica_groups=mesh['clip'=2,'ha'=8,'ta'=2] {'ha','ta'}, use_global_device_ids=true, to_apply=%region_5.6 | all-reduce | flops 32 | bytes 256 | tf_op jit(solution)/shard_map/psum | solution.py:111
  96.4 1.9 %fusion = bf16[6,4,128,384]{3,2,1,0:T(8,128)(2,1)S(1)} fusion(bf16[6,4,128,384]{3,2,1,0:T(8,128)(2,1)S(1)} %bitcast.53, f32[384]{0:T(512)S(1)} %copy-done.11, f32[384]{0:T(512)S(1)} %copy-done.12, f32[384]{0:T(512)S(1)} %mul.34, f32[384]{0:T(512)S(1)} %sub.26, pred[6,4]{1,0:T(8,128)(4,1)S(1)} %and_and_fusion), kind=kLoop, calls=%fused_computation.5 | loop fusion | flops 12976128 | bytes 4724760 | tf_op jit(solution)/shard_map/jit(_where)/select_n | solution.py:120
  98.3 3.6 %pad_slice_fusion.18 = (bf16[4,2,128,384]{3,2,1,0:T(8,128)(2,1)S(1)}, bf16[4,2,128,384]{3,2,1,0:T(8,128)(2,1)S(1)}, bf16[4,2,128,384]{3,2,1,0:T(8,128)(2,1)S(1)}...) fusion(bf16[6,4,128,384]{3,2,1,0:T(8,128)(2,1)S(1)} %fusion), kind=kLoop, calls=%fused_computation.76 | loop fusion | bytes 13369344 | tf_op jit(solution)/shard_map/slice | solution.py:63
  101.9 0.7 fusion.26
  102.6 3.8 %pad_slice_fusion.19 = (bf16[4,2,128,384]{3,2,1,0:T(8,128)(2,1)S(1)}, bf16[4,2,128,384]{3,2,1,0:T(8,128)(2,1)S(1)}, bf16[4,2,128,384]{3,2,1,0:T(8,128)(2,1)S(1)}...) fusion(bf16[6,4,128,384]{3,2,1,0:T(8,128)(2,1)S(1)} %fusion), kind=kLoop, calls=%fused_computation.77 | loop fusion | bytes 11010048 | tf_op jit(solution)/shard_map/slice | solution.py:63
  106.4 0.3 pad_maximum_fusion.7
  106.7 0.9 copy-done.10
  107.6 1.4 %fusion.34 = f32[1024,384]{1,0:T(8,128)S(1)} fusion(bf16[1024,1152]{1,0:T(8,128)(2,1)S(1)} %bitcast.55, bf16[1152,384]{1,0:T(8,128)(2,1)S(1)} %bitcast.72), kind=kOutput, calls=%fused_computation.103 | convolution fusion | flops 905969664 | bytes 4816896 | tf_op jit(solution)/shard_map/dot_general | solution.py:72
  109.0 0.3 pad_maximum_fusion.6
  109.3 0.9 copy-done.9
  110.2 1.4 %fusion.33 = f32[1024,384]{1,0:T(8,128)S(1)} fusion(bf16[1024,1152]{1,0:T(8,128)(2,1)S(1)} %bitcast.56, bf16[1152,384]{1,0:T(8,128)(2,1)S(1)} %bitcast.71), kind=kOutput, calls=%fused_computation.102 | convolution fusion | flops 905969664 | bytes 4816896 | tf_op jit(solution)/shard_map/dot_general | solution.py:72
  111.6 0.3 pad_maximum_fusion.5
  111.9 0.9 copy-done.8
  112.8 1.4 %fusion.32 = f32[1024,384]{1,0:T(8,128)S(1)} fusion(bf16[1024,1152]{1,0:T(8,128)(2,1)S(1)} %bitcast.57, bf16[1152,384]{1,0:T(8,128)(2,1)S(1)} %bitcast.70), kind=kOutput, calls=%fused_computation.101 | convolution fusion | flops 905969664 | bytes 4816896 | tf_op jit(solution)/shard_map/dot_general | solution.py:72
  114.2 0.3 pad_maximum_fusion.4
  114.5 0.9 copy-done.7
  115.4 1.4 %fusion.31 = f32[1024,384]{1,0:T(8,128)S(1)} fusion(bf16[1024,1152]{1,0:T(8,128)(2,1)S(1)} %bitcast.58, bf16[1152,384]{1,0:T(8,128)(2,1)S(1)} %bitcast.69), kind=kOutput, calls=%fused_computation.100 | convolution fusion | flops 905969664 | bytes 4816896 | tf_op jit(solution)/shard_map/dot_general | solution.py:72
  116.9 0.3 pad_maximum_fusion.3
  117.2 0.9 copy-done.6
  118.0 1.4 %fusion.30 = f32[1024,384]{1,0:T(8,128)S(1)} fusion(bf16[1024,1152]{1,0:T(8,128)(2,1)S(1)} %bitcast.59, bf16[1152,384]{1,0:T(8,128)(2,1)S(1)} %bitcast.68), kind=kOutput, calls=%fused_computation.99 | convolution fusion | flops 905969664 | bytes 4816896 | tf_op jit(solution)/shard_map/dot_general | solution.py:72
  119.5 0.3 pad_maximum_fusion.2
  119.8 0.9 copy-done.5
  120.6 1.4 %fusion.29 = f32[1024,384]{1,0:T(8,128)S(1)} fusion(bf16[1024,1152]{1,0:T(8,128)(2,1)S(1)} %bitcast.60, bf16[1152,384]{1,0:T(8,128)(2,1)S(1)} %bitcast.67), kind=kOutput, calls=%fused_computation.98 | convolution fusion | flops 905969664 | bytes 4816896 | tf_op jit(solution)/shard_map/dot_general | solution.py:72
  122.1 0.3 pad_maximum_fusion
  122.4 0.9 copy-done.4
  123.2 1.4 %fusion.27 = f32[1024,384]{1,0:T(8,128)S(1)} fusion(bf16[1024,1152]{1,0:T(8,128)(2,1)S(1)} %bitcast.61, bf16[1152,384]{1,0:T(8,128)(2,1)S(1)} %bitcast.66), kind=kOutput, calls=%fused_computation.96 | convolution fusion | flops 905969664 | bytes 4816896 | tf_op jit(solution)/shard_map/dot_general | solution.py:72
  124.7 0.3 pad_maximum_fusion.1
  125.0 0.9 copy-done.3
  125.8 1.4 %fusion.28 = f32[1024,384]{1,0:T(8,128)S(1)} fusion(bf16[1024,1152]{1,0:T(8,128)(2,1)S(1)} %bitcast.62, bf16[1152,384]{1,0:T(8,128)(2,1)S(1)} %bitcast.65), kind=kOutput, calls=%fused_computation.97 | convolution fusion | flops 905969664 | bytes 4816896 | tf_op jit(solution)/shard_map/dot_general | solution.py:72
  127.3 0.3 pad_maximum_fusion.8
  127.6 0.9 copy-done.2
  128.5 1.7 %add_add_fusion = f32[1024,384]{1,0:T(8,128)S(1)} fusion(f32[1024,384]{1,0:T(8,128)S(1)} %fusion.34, f32[1024,384]{1,0:T(8,128)S(1)} %fusion.33, f32[1024,384]{1,0:T(8,128)S(1)} %fusion.32, f32[1024,384]{1,0:T(8,128)S(1)} %fusion.31, f32[1024,384]{1,0:T(8,128)S(1)} %fusion.30, f32[1024,384]{1,0:T(8,128)S(1)} %fusion.29, f32[1024,384]{1,0:T(8,128)S(1)} %fusion.27, ...), kind=kOutput, calls=%fused_computation.19 | convolution fusion | flops 909115392 | bytes 17399808 | tf_op jit(solution)/shard_map/dot_general | solution.py:72
  130.2 1.1 fusion.4
  (71 shorter events, 3.8 us)
Async XLA Ops:
  0.0 28.7 %copy-start = (bf16[3,3,3,16,384]{4,3,2,1,0:T(8,128)(2,1)S(1)}, bf16[3,3,3,16,384]{4,3,2,1,0:T(8,128)(2,1)}, u32[]{:S(2)}) copy-start(bf16[3,3,3,16,384]{4,3,2,1,0:T(8,128)(2,1)} %param.8) | copy-start | bytes 995332
  5.3 8.0 %collective-permute-start = (bf16[4,2,128,16]{3,2,1,0:T(8,128)(2,1)S(1)}, bf16[4,2,128,16]{3,2,1,0:T(8,128)(2,1)S(1)}, u32[]{:S(2)}, u32[]{:S(2)}) collective-permute-start(bf16[4,2,128,16]{3,2,1,0:T(8,128)(2,1)S(1)} %bitcast.63), channel_id=1, source_target_pairs={{0,1},{2,3},{4,5},{6,7},{8,9},{10,11},{12,13},{14,15},{16,17},{18,... | collective-permute-start | bytes 98312 | tf_op jit(solution)/shard_map/ppermute | solution.py:15
  13.4 7.1 %collective-permute-start.2 = (bf16[8,2,128,16]{2,3,1,0:T(8,128)(2,1)S(1)}, bf16[8,2,128,16]{2,3,1,0:T(8,128)(2,1)S(1)}, u32[]{:S(2)}, u32[]{:S(2)}) collective-permute-start(bf16[8,2,128,16]{2,3,1,0:T(8,128)(2,1)S(1)} %pad_maximum_fusion.11), channel_id=1, source_target_pairs={{2,0},{4,2},{6,4},{8,6},{10,8},{12,10},{14,12},{3,1},{5,3},{7,5},{... | collective-permute-start | bytes 196616 | tf_op jit(solution)/shard_map/ppermute | solution.py:26
  14.7 7.4 %collective-permute-start.1 = (bf16[8,2,128,16]{2,3,1,0:T(8,128)(2,1)S(1)}, bf16[8,2,128,16]{2,3,1,0:T(8,128)(2,1)S(1)}, u32[]{:S(2)}, u32[]{:S(2)}) collective-permute-start(bf16[8,2,128,16]{2,3,1,0:T(8,128)(2,1)S(1)} %pad_maximum_fusion.11), channel_id=1, source_target_pairs={{0,2},{2,4},{4,6},{6,8},{8,10},{10,12},{12,14},{1,3},{3,5},{5,7},{... | collective-permute-start | bytes 196616 | tf_op jit(solution)/shard_map/ppermute | solution.py:25
  25.5 3.2 %copy-start.14 = (f32[384]{0:T(512)S(1)}, f32[384]{0:T(512)}, u32[]{:S(2)}) copy-start(f32[384]{0:T(512)} %param.9) | copy-start | bytes 4612
  32.3 64.0 %copy-start.11 = (f32[384]{0:T(512)S(1)}, f32[384]{0:T(512)}, u32[]{:S(2)}) copy-start(f32[384]{0:T(512)} %param.11) | copy-start | bytes 4612
  32.3 64.0 %copy-start.12 = (f32[384]{0:T(512)S(1)}, f32[384]{0:T(512)}, u32[]{:S(2)}) copy-start(f32[384]{0:T(512)} %param.10) | copy-start | bytes 4612
  106.4 1.2 copy-start.10
  109.0 1.2 copy-start.9
  111.6 1.2 copy-start.8
  114.2 1.2 copy-start.7
  116.8 1.2 copy-start.6
  119.5 1.2 copy-start.5
  122.1 1.2 copy-start.4
  124.7 1.2 copy-start.3
  127.3 1.2 copy-start.2
  128.5 1.8 %copy-start.13 = (f32[384]{0:T(512)S(1)}, f32[384]{0:T(512)}, u32[]{:S(2)}) copy-start(f32[384]{0:T(512)} %param.13) | copy-start | bytes 4612
  128.5 2.9 %copy-start.1 = (bf16[3,3,3,16,384]{4,3,2,1,0:T(8,128)(2,1)S(1)}, bf16[3,3,3,16,384]{4,3,2,1,0:T(8,128)(2,1)}, u32[]{:S(2)}) copy-start(bf16[3,3,3,16,384]{4,3,2,1,0:T(8,128)(2,1)} %param.8) | copy-start | bytes 995332
where the time goes:
time: 132 us; the launch traced here: 131 us
  blocking collectives  66.4 us (50%)
  local copies, waits for them, and re-layouts  30.3 us (23%)
  matrix products  16.8 us (13%)
  starting transfers between devices  8.88 us (7%)
  other arithmetic  6.55 us (5%)
  waiting for transfers between devices  1.81 us (1%)
    psum x1, blocking collectives, body(): mean = lax.psum(group_totals(values), ('ha', 'ta')) / count  32.9 us
    psum x1, blocking collectives, body(): var = lax.psum(group_totals(centered * centered), ('ha', 'ta')) / count  29.7 us
    dot_general x9, matrix products, middle_conv(): jnp.dot(slab, w_mid[frame_tap, row_tap].reshape(3 * channels, -1), prefer...  13.2 us
    unnamed x58, local copies, waits for them, and re-layouts  10.8 us
    slice x3, local copies, waits for them, and re-layouts, middle_conv(): padded[frame_tap:frame_tap + frames, row_tap:row_tap + rows, col_tap:col_...  8.12 us
    slice x1, local copies, waits for them, and re-layouts, middle_conv(): w_mid[frame_tap, row_tap].reshape(3 * channels, -1)  5.75 us
    ppermute x1, starting transfers between devices, extended_2(): before = lax.ppermute(last, axis, up)  5.5 us
    all_to_all x1, blocking collectives, body(): lax.all_to_all(latent_tokens, 'ta', split_axis=0, concat_axis=1, tiled=True)  3.75 us
  transfers between devices with their start and end apart: 3, of which 2 were waited for; matrix products, arithmetic and copies ran while one was open for 5% of the time, Pallas kernels for 0%

commit v1 on v0

--- a/solution.py
+++ b/solution.py
@@ -106,7 +106,7 @@
     values = lax.optimization_barrier(hidden).astype(jnp.float32)
     members = values.shape[-1] // GROUPS
     count = float(lax.axis_size("ha") * lax.axis_size("ta") * frames * rows * cols * members)
-    mean = lax.psum(group_totals(values), ("ha", "ta")) / count
+    mean = lax.psum(lax.psum(group_totals(values), "ta"), "ha") / count
     centered = values - jnp.repeat(mean, members)
     var = lax.psum(group_totals(centered * centered), ("ha", "ta")) / count
     active = normalize(wide_hidden, mean, var, gn_gain, gn_shift)

time: 132 us -> 125 us (0.947)
  blocking collectives: 66.4 us -> 58.9 us
    psum x1 -> x2, blocking collectives: 32.9 us -> 25.5 us  [body(): mean = lax.psum(lax.psum(group_totals(values), 'ta'), 'ha') / count]
where the time goes in v1:
time: 125 us; the launch traced here: 124 us
  blocking collectives  58.9 us (47%)
  local copies, waits for them, and re-layouts  30.3 us (24%)
  matrix products  16.8 us (13%)
  starting transfers between devices  8.88 us (7%)
  other arithmetic  6.55 us (5%)
  waiting for transfers between devices  1.81 us (1%)
    psum x1, blocking collectives, body(): var = lax.psum(group_totals(centered * centered), ('ha', 'ta')) / count  29.7 us
    psum x2, blocking collectives, body(): mean = lax.psum(lax.psum(group_totals(values), 'ta'), 'ha') / count  25.5 us
    dot_general x9, matrix products, middle_conv(): jnp.dot(slab, w_mid[frame_tap, row_tap].reshape(3 * channels, -1), prefer...  13.2 us
    unnamed x58, local copies, waits for them, and re-layouts  10.8 us
    slice x3, local copies, waits for them, and re-layouts, middle_conv(): padded[frame_tap:frame_tap + frames, row_tap:row_tap + rows, col_tap:col_...  8.12 us
    slice x1, local copies, waits for them, and re-layouts, middle_conv(): w_mid[frame_tap, row_tap].reshape(3 * channels, -1)  5.74 us
    ppermute x1, starting transfers between devices, extended_2(): before = lax.ppermute(last, axis, up)  5.5 us
    all_to_all x1, blocking collectives, body(): lax.all_to_all(latent_tokens, 'ta', split_axis=0, concat_axis=1, tiled=True)  3.75 us
  transfers between devices with their start and end apart: 3, of which 2 were waited for; matrix products, arithmetic and copies ran while one was open for 5% of the time, Pallas kernels for 0%

profile of v1, /device:TPU:0, one launch (start us, length us, event | category | flops | bytes accessed | tf_op | source)
XLA Modules:
  0.0 123.9 jit_solution(14839199736923180877)
XLA Ops:
  0.0 1.0 reshape.124
  1.0 3.7 %all_to_all.15 = bf16[2,2,4096]{2,1,0:T(2,128)(2,1)S(1)} all-to-all(bf16[2,2,4096]{2,1,0:T(2,128)(2,1)S(1)} %reshape.124), channel_id=1, replica_groups=mesh['clip'=2,'ha'=8,'ta'=2] {'ta'}, dimensions={0} | all-to-all | bytes 65536 | tf_op jit(solution)/shard_map/all_to_all | solution.py:96
  5.3 2.1 %collective-permute-start = (bf16[4,2,128,16]{3,2,1,0:T(8,128)(2,1)S(1)}, bf16[4,2,128,16]{3,2,1,0:T(8,128)(2,1)S(1)}, u32[]{:S(2)}, u32[]{:S(2)}) collective-permute-start(bf16[4,2,128,16]{3,2,1,0:T(8,128)(2,1)S(1)} %bitcast.63), channel_id=1, source_target_pairs={{0,1},{2,3},{4,5},{6,7},{8,9},{10,11},{12,13},{14,15},{16,17},{18,... | collective-permute-start | bytes 98312 | tf_op jit(solution)/shard_map/ppermute | solution.py:15
  7.4 5.7 %fusion.25 = (bf16[1,1,3,384,384]{4,3,2,1,0:T(8,128)(2,1)}, bf16[1,1,3,384,384]{4,3,2,1,0:T(8,128)(2,1)}, bf16[1,1,3,384,384]{4,3,2,1,0:T(8,128)(2,1)}, bf16[1,1...) fusion(bf16[3,3,3,384,384]{4,3,2,1,0:T(8,128)(2,1)} %param.12), kind=kLoop, calls=%fused_computation.94 | loop fusion | bytes 15925248 | tf_op jit(solution)/shard_map/slice | solution.py:74
  13.4 1.3 %collective-permute-start.2 = (bf16[8,2,128,16]{2,3,1,0:T(8,128)(2,1)S(1)}, bf16[8,2,128,16]{2,3,1,0:T(8,128)(2,1)S(1)}, u32[]{:S(2)}, u32[]{:S(2)}) collective-permute-start(bf16[8,2,128,16]{2,3,1,0:T(8,128)(2,1)S(1)} %pad_maximum_fusion.11), channel_id=1, source_target_pairs={{2,0},{4,2},{6,4},{8,6},{10,8},{12,10},{14,12},{3,1},{5,3},{7,5},{... | collective-permute-start | bytes 196616 | tf_op jit(solution)/shard_map/ppermute | solution.py:26
  14.7 5.5 %collective-permute-start.1 = (bf16[8,2,128,16]{2,3,1,0:T(8,128)(2,1)S(1)}, bf16[8,2,128,16]{2,3,1,0:T(8,128)(2,1)S(1)}, u32[]{:S(2)}, u32[]{:S(2)}) collective-permute-start(bf16[8,2,128,16]{2,3,1,0:T(8,128)(2,1)S(1)} %pad_maximum_fusion.11), channel_id=1, source_target_pairs={{0,2},{2,4},{4,6},{6,8},{8,10},{10,12},{12,14},{1,3},{3,5},{5,7},{... | collective-permute-start | bytes 196616 | tf_op jit(solution)/shard_map/ppermute | solution.py:25
  20.3 0.2 collective-permute-done.2
  20.6 1.6 %collective-permute-done.1 = bf16[8,2,128,16]{2,3,1,0:T(8,128)(2,1)S(1)} collective-permute-done((bf16[8,2,128,16]{2,3,1,0:T(8,128)(2,1)S(1)}, bf16[8,2,128,16]{2,3,1,0:T(8,128)(2,1)S(1)}, u32[]{:S(2)}, u32[]{:S(2)}) %collective-permute-start.1) | collective-permute-done | bytes 65568 | tf_op jit(solution)/shard_map/ppermute | solution.py:25
  24.5 1.0 copy.18
  25.5 3.1 %reshape.112 = bf16[3072,432]{0,1:T(8,128)(2,1)} reshape(bf16[6,4,128,432]{2,1,0,3:T(4,128)(2,1)S(1)} %copy.18) | data formatting | bytes 5308416 | tf_op jit(solution)/shard_map/reshape | solution.py:49
  28.7 3.6 %add_convert_fusion = bf16[3072,384]{1,0:T(8,128)(2,1)S(1)} fusion(bf16[3072,432]{0,1:T(8,128)(2,1)} %reshape.112, bf16[432,384]{1,0:T(8,128)(2,1)S(1)} %bitcast.49, f32[384]{0:T(512)S(1)} %copy-done.14), kind=kOutput, calls=%fused_computation.1 | convolution fusion | flops 1021575168 | bytes 5346816 | tf_op jit(solution)/shard_map/dot_general | solution.py:50
  32.4 0.2 convert_reduce_fusion
  32.8 2.5 %psum.21 = f32[32]{0:T(128)S(1)} all-reduce(f32[32]{0:T(128)S(1)} %reduce_sum.25), channel_id=1, replica_groups=mesh['clip'=2,'ha'=8,'ta'=2] {'ta'}, use_global_device_ids=true, to_apply=%region_2.3 | all-reduce | flops 32 | bytes 256 | tf_op jit(solution)/shard_map/psum | solution.py:109
  35.3 23.0 %psum.22 = f32[32]{0:T(128)S(1)} all-reduce(f32[32]{0:T(128)S(1)} %psum.21), channel_id=1, replica_groups=mesh['clip'=2,'ha'=8,'ta'=2] {'ha'}, use_global_device_ids=true, to_apply=%region_3.4 | all-reduce | flops 32 | bytes 256 | tf_op jit(solution)/shard_map/psum | solution.py:109
  58.5 0.3 fusion.2
  59.0 29.7 %psum.23 = f32[32]{0:T(128)S(1)} all-reduce(f32[32]{0:T(128)S(1)} %reduce_sum.37), channel_id=1, replica_groups=mesh['clip'=2,'ha'=8,'ta'=2] {'ha','ta'}, use_global_device_ids=true, to_apply=%region_6.7 | all-reduce | flops 32 | bytes 256 | tf_op jit(solution)/shard_map/psum | solution.py:111
  88.9 1.9 %fusion = bf16[6,4,128,384]{3,2,1,0:T(8,128)(2,1)S(1)} fusion(bf16[6,4,128,384]{3,2,1,0:T(8,128)(2,1)S(1)} %bitcast.53, f32[384]{0:T(512)S(1)} %copy-done.11, f32[384]{0:T(512)S(1)} %copy-done.12, f32[384]{0:T(512)S(1)} %mul.34, f32[384]{0:T(512)S(1)} %sub.26, pred[6,4]{1,0:T(8,128)(4,1)S(1)} %and_and_fusion), kind=kLoop, calls=%fused_computation.5 | loop fusion | flops 12976128 | bytes 4724760 | tf_op jit(solution)/shard_map/jit(_where)/select_n | solution.py:120
  90.8 3.6 %pad_slice_fusion.18 = (bf16[4,2,128,384]{3,2,1,0:T(8,128)(2,1)S(1)}, bf16[4,2,128,384]{3,2,1,0:T(8,128)(2,1)S(1)}, bf16[4,2,128,384]{3,2,1,0:T(8,128)(2,1)S(1)}...) fusion(bf16[6,4,128,384]{3,2,1,0:T(8,128)(2,1)S(1)} %fusion), kind=kLoop, calls=%fused_computation.76 | loop fusion | bytes 13369344 | tf_op jit(solution)/shard_map/slice | solution.py:63
  94.4 0.7 fusion.26
  95.1 3.8 %pad_slice_fusion.19 = (bf16[4,2,128,384]{3,2,1,0:T(8,128)(2,1)S(1)}, bf16[4,2,128,384]{3,2,1,0:T(8,128)(2,1)S(1)}, bf16[4,2,128,384]{3,2,1,0:T(8,128)(2,1)S(1)}...) fusion(bf16[6,4,128,384]{3,2,1,0:T(8,128)(2,1)S(1)} %fusion), kind=kLoop, calls=%fused_computation.77 | loop fusion | bytes 11010048 | tf_op jit(solution)/shard_map/slice | solution.py:63
  98.9 0.3 pad_maximum_fusion.7
  99.2 0.9 copy-done.10
  100.1 1.4 %fusion.34 = f32[1024,384]{1,0:T(8,128)S(1)} fusion(bf16[1024,1152]{1,0:T(8,128)(2,1)S(1)} %bitcast.55, bf16[1152,384]{1,0:T(8,128)(2,1)S(1)} %bitcast.72), kind=kOutput, calls=%fused_computation.103 | convolution fusion | flops 905969664 | bytes 4816896 | tf_op jit(solution)/shard_map/dot_general | solution.py:72
  101.6 0.3 pad_maximum_fusion.6
  101.9 0.9 copy-done.9
  102.7 1.4 %fusion.33 = f32[1024,384]{1,0:T(8,128)S(1)} fusion(bf16[1024,1152]{1,0:T(8,128)(2,1)S(1)} %bitcast.56, bf16[1152,384]{1,0:T(8,128)(2,1)S(1)} %bitcast.71), kind=kOutput, calls=%fused_computation.102 | convolution fusion | flops 905969664 | bytes 4816896 | tf_op jit(solution)/shard_map/dot_general | solution.py:72
  104.2 0.3 pad_maximum_fusion.5
  104.5 0.9 copy-done.8
  105.3 1.4 %fusion.32 = f32[1024,384]{1,0:T(8,128)S(1)} fusion(bf16[1024,1152]{1,0:T(8,128)(2,1)S(1)} %bitcast.57, bf16[1152,384]{1,0:T(8,128)(2,1)S(1)} %bitcast.70), kind=kOutput, calls=%fused_computation.101 | convolution fusion | flops 905969664 | bytes 4816896 | tf_op jit(solution)/shard_map/dot_general | solution.py:72
  106.8 0.3 pad_maximum_fusion.4
  107.1 0.9 copy-done.7
  107.9 1.4 %fusion.31 = f32[1024,384]{1,0:T(8,128)S(1)} fusion(bf16[1024,1152]{1,0:T(8,128)(2,1)S(1)} %bitcast.58, bf16[1152,384]{1,0:T(8,128)(2,1)S(1)} %bitcast.69), kind=kOutput, calls=%fused_computation.100 | convolution fusion | flops 905969664 | bytes 4816896 | tf_op jit(solution)/shard_map/dot_general | solution.py:72
  109.4 0.3 pad_maximum_fusion.3
  109.7 0.9 copy-done.6
  110.5 1.4 %fusion.30 = f32[1024,384]{1,0:T(8,128)S(1)} fusion(bf16[1024,1152]{1,0:T(8,128)(2,1)S(1)} %bitcast.59, bf16[1152,384]{1,0:T(8,128)(2,1)S(1)} %bitcast.68), kind=kOutput, calls=%fused_computation.99 | convolution fusion | flops 905969664 | bytes 4816896 | tf_op jit(solution)/shard_map/dot_general | solution.py:72
  112.0 0.3 pad_maximum_fusion.2
  112.3 0.9 copy-done.5
  113.2 1.4 %fusion.29 = f32[1024,384]{1,0:T(8,128)S(1)} fusion(bf16[1024,1152]{1,0:T(8,128)(2,1)S(1)} %bitcast.60, bf16[1152,384]{1,0:T(8,128)(2,1)S(1)} %bitcast.67), kind=kOutput, calls=%fused_computation.98 | convolution fusion | flops 905969664 | bytes 4816896 | tf_op jit(solution)/shard_map/dot_general | solution.py:72
  114.6 0.3 pad_maximum_fusion
  114.9 0.9 copy-done.4
  115.8 1.4 %fusion.27 = f32[1024,384]{1,0:T(8,128)S(1)} fusion(bf16[1024,1152]{1,0:T(8,128)(2,1)S(1)} %bitcast.61, bf16[1152,384]{1,0:T(8,128)(2,1)S(1)} %bitcast.66), kind=kOutput, calls=%fused_computation.96 | convolution fusion | flops 905969664 | bytes 4816896 | tf_op jit(solution)/shard_map/dot_general | solution.py:72
  117.2 0.3 pad_maximum_fusion.1
  117.5 0.9 copy-done.3
  118.4 1.4 %fusion.28 = f32[1024,384]{1,0:T(8,128)S(1)} fusion(bf16[1024,1152]{1,0:T(8,128)(2,1)S(1)} %bitcast.62, bf16[1152,384]{1,0:T(8,128)(2,1)S(1)} %bitcast.65), kind=kOutput, calls=%fused_computation.97 | convolution fusion | flops 905969664 | bytes 4816896 | tf_op jit(solution)/shard_map/dot_general | solution.py:72
  119.8 0.3 pad_maximum_fusion.8
  120.1 0.9 copy-done.2
  121.0 1.7 %add_add_fusion = f32[1024,384]{1,0:T(8,128)S(1)} fusion(f32[1024,384]{1,0:T(8,128)S(1)} %fusion.34, f32[1024,384]{1,0:T(8,128)S(1)} %fusion.33, f32[1024,384]{1,0:T(8,128)S(1)} %fusion.32, f32[1024,384]{1,0:T(8,128)S(1)} %fusion.31, f32[1024,384]{1,0:T(8,128)S(1)} %fusion.30, f32[1024,384]{1,0:T(8,128)S(1)} %fusion.29, f32[1024,384]{1,0:T(8,128)S(1)} %fusion.27, ...), kind=kOutput, calls=%fused_computation.19 | convolution fusion | flops 909115392 | bytes 17399808 | tf_op jit(solution)/shard_map/dot_general | solution.py:72
  122.7 1.1 fusion.4
  (72 shorter events, 4.0 us)
Async XLA Ops:
  0.0 28.7 %copy-start = (bf16[3,3,3,16,384]{4,3,2,1,0:T(8,128)(2,1)S(1)}, bf16[3,3,3,16,384]{4,3,2,1,0:T(8,128)(2,1)}, u32[]{:S(2)}) copy-start(bf16[3,3,3,16,384]{4,3,2,1,0:T(8,128)(2,1)} %param.8) | copy-start | bytes 995332
  5.3 8.0 %collective-permute-start = (bf16[4,2,128,16]{3,2,1,0:T(8,128)(2,1)S(1)}, bf16[4,2,128,16]{3,2,1,0:T(8,128)(2,1)S(1)}, u32[]{:S(2)}, u32[]{:S(2)}) collective-permute-start(bf16[4,2,128,16]{3,2,1,0:T(8,128)(2,1)S(1)} %bitcast.63), channel_id=1, source_target_pairs={{0,1},{2,3},{4,5},{6,7},{8,9},{10,11},{12,13},{14,15},{16,17},{18,... | collective-permute-start | bytes 98312 | tf_op jit(solution)/shard_map/ppermute | solution.py:15
  13.4 7.1 %collective-permute-start.2 = (bf16[8,2,128,16]{2,3,1,0:T(8,128)(2,1)S(1)}, bf16[8,2,128,16]{2,3,1,0:T(8,128)(2,1)S(1)}, u32[]{:S(2)}, u32[]{:S(2)}) collective-permute-start(bf16[8,2,128,16]{2,3,1,0:T(8,128)(2,1)S(1)} %pad_maximum_fusion.11), channel_id=1, source_target_pairs={{2,0},{4,2},{6,4},{8,6},{10,8},{12,10},{14,12},{3,1},{5,3},{7,5},{... | collective-permute-start | bytes 196616 | tf_op jit(solution)/shard_map/ppermute | solution.py:26
  14.7 7.4 %collective-permute-start.1 = (bf16[8,2,128,16]{2,3,1,0:T(8,128)(2,1)S(1)}, bf16[8,2,128,16]{2,3,1,0:T(8,128)(2,1)S(1)}, u32[]{:S(2)}, u32[]{:S(2)}) collective-permute-start(bf16[8,2,128,16]{2,3,1,0:T(8,128)(2,1)S(1)} %pad_maximum_fusion.11), channel_id=1, source_target_pairs={{0,2},{2,4},{4,6},{6,8},{8,10},{10,12},{12,14},{1,3},{3,5},{5,7},{... | collective-permute-start | bytes 196616 | tf_op jit(solution)/shard_map/ppermute | solution.py:25
  25.5 3.2 %copy-start.14 = (f32[384]{0:T(512)S(1)}, f32[384]{0:T(512)}, u32[]{:S(2)}) copy-start(f32[384]{0:T(512)} %param.9) | copy-start | bytes 4612
  32.3 56.6 %copy-start.11 = (f32[384]{0:T(512)S(1)}, f32[384]{0:T(512)}, u32[]{:S(2)}) copy-start(f32[384]{0:T(512)} %param.11) | copy-start | bytes 4612
  32.3 56.6 %copy-start.12 = (f32[384]{0:T(512)S(1)}, f32[384]{0:T(512)}, u32[]{:S(2)}) copy-start(f32[384]{0:T(512)} %param.10) | copy-start | bytes 4612
  98.9 1.2 copy-start.10
  101.5 1.2 copy-start.9
  104.2 1.2 copy-start.8
  106.8 1.2 copy-start.7
  109.4 1.2 copy-start.6
  112.0 1.2 copy-start.5
  114.6 1.2 copy-start.4
  117.2 1.2 copy-start.3
  119.8 1.2 copy-start.2
  121.0 1.8 %copy-start.13 = (f32[384]{0:T(512)S(1)}, f32[384]{0:T(512)}, u32[]{:S(2)}) copy-start(f32[384]{0:T(512)} %param.13) | copy-start | bytes 4612
  121.0 2.9 %copy-start.1 = (bf16[3,3,3,16,384]{4,3,2,1,0:T(8,128)(2,1)S(1)}, bf16[3,3,3,16,384]{4,3,2,1,0:T(8,128)(2,1)}, u32[]{:S(2)}) copy-start(bf16[3,3,3,16,384]{4,3,2,1,0:T(8,128)(2,1)} %param.8) | copy-start | bytes 995332
